TPU v7x, 32 devices: a whole 2x2x4 slice. The times are simulated.
32 devices in a mesh: dom: 8 (over y, x, core), feat: 4 (over z).
Axes of the slice: x: 2, y: 2, z: 4, core: 2. Of those that a mesh axis runs over, the one named last changes fastest.
Arguments:
- features: bfloat16 [512, 65536], P('feat', 'dom'), may hold values from -3 to 3
- send_blocks: int32 [8, 8, 8], P('dom'), may hold values from 0 to 63, as said below
- counts: int32 [8, 8], P('dom'), may hold values from 0 to 8, as said below
- tile_blocks: int32 [24, 512], P(None, 'dom'), may hold values from 0 to 127, as said below
- neighbours: int32 [24, 65536], P(None, 'dom'), may hold values from 0 to 127
- degree: int32 [65536], P('dom'), may hold values from 1 to 24
- epsilon: float32 [1], replicated, may hold values from -0.3 to 0.6
- w_first: bfloat16 [512, 512], replicated, may hold values from -0.25 to 0.25
- b_first: float32 [512], replicated, may hold values from -3 to 3
- w_second: bfloat16 [512, 512], replicated, may hold values from -0.25 to 0.25
- b_second: float32 [512], replicated, may hold values from -3 to 3
Outputs:
- updated: bfloat16 [65536, 512], P(('dom', 'feat'))
Inputs may be any that keep to these rules, and one draw needn't show every extreme that they name: `send_blocks`: entry [q, p, s] is a row block of partition q; the entries of one pair (q, p) are distinct. counts[q, p] leading slots of send_blocks[q, p] are used; zero where q == p; in every draw some partition receives 8 blocks from every other partition. `tile_blocks`: an entry for a row block of partition p is below 64 (a row block of p) or equals 64 + q * 8 + s for a slot s of a partition q other than p.
All inputs are finite; a program needn't handle non-finite values.
Results may differ from a plain program's by a relative error of at most 0.0055.
Values may be sent and summed in bfloat16 or wider, within the bound.
A program may use at most 64 MiB of HBM per device.

v0:
```python
import functools

import jax
import jax.numpy as jnp
from jax import lax
from jax.experimental import pallas as pl
from jax.experimental.pallas import tpu as pltpu
from jax.sharding import PartitionSpec as P

BLOCK = 128
SUBLANES = 16
PIECES = 4


def chunk_widths(cols):
    widths = []
    while sum(widths) < cols:
        widths.append(min(max(SUBLANES, sum(widths)), cols - sum(widths)))
    return widths


def kernel(
    parts, groups, pieces, widths,
    sb_ref, cnt_ref, tile_ref, eps_ref, deg_ref, b1_ref, b2_ref,
    feat_hbm, nbr_hbm, w1_hbm, w2_hbm,
    out_ref,
    *scratch,
):
    chunks = len(widths)
    starts = [sum(widths[:c]) for c in range(chunks)]
    tables, locals_, stages, feats = (scratch[i * chunks:(i + 1) * chunks] for i in range(4))
    (nbr_ref, w1_ref, w2_ref, zstage, parcel,
     hsend, hrecv, zsend, zrecv, in_sem) = scratch[4 * chunks:]
    me = lax.axis_index("dom")
    z = lax.axis_index("feat")
    slots = stages[0].shape[1]
    list_width, block_count = tile_ref.shape
    per_piece = block_count // groups // pieces
    piece_nodes = per_piece * BLOCK
    half = groups // 2

    def lanes(block):
        return pl.ds(pl.multiple_of(block * BLOCK, BLOCK), BLOCK)

    def halo_copy(c, peer, source):
        return pltpu.make_async_remote_copy(
            src_ref=stages[c].at[peer],
            dst_ref=tables[c].at[pl.ds(block_count + source * slots, slots)],
            send_sem=hsend.at[c, peer],
            recv_sem=hrecv.at[c, source],
            device_id={"dom": peer},
            device_id_type=pl.DeviceIdType.MESH,
        )

    def row_copy(c, p, dest, source):
        span = pl.ds(starts[c], widths[c])
        return pltpu.make_async_remote_copy(
            src_ref=zstage.at[p, dest, span],
            dst_ref=parcel.at[p, source, span],
            send_sem=zsend.at[c, p, dest],
            recv_sem=zrecv.at[c, p, source],
            device_id={"feat": dest},
            device_id_type=pl.DeviceIdType.MESH,
        )

    def dest_of(k):
        if k < half:
            return lax.rem(z // half + 1, 2) * half + lax.rem(lax.rem(z, half) + k, half)
        return (z // half) * half + lax.rem(lax.rem(z, half) + (k - half + 1), half)

    barrier = pltpu.get_barrier_semaphore()

    @pl.loop(1, parts)
    def _(k):
        pl.semaphore_signal(
            barrier, inc=1, device_id={"dom": lax.rem(me + k, parts)},
            device_id_type=pl.DeviceIdType.MESH,
        )

    @pl.loop(1, groups)
    def _(k):
        pl.semaphore_signal(
            barrier, inc=1, device_id={"feat": lax.rem(z + k, groups)},
            device_id_type=pl.DeviceIdType.MESH,
        )

    loads = [
        pltpu.make_async_copy(
            feat_hbm.at[pl.ds(starts[c], widths[c])], feats[c], in_sem.at[c]
        )
        for c in range(chunks)
    ]
    loads.append(pltpu.make_async_copy(nbr_hbm, nbr_ref, in_sem.at[chunks]))
    loads.append(pltpu.make_async_copy(w1_hbm, w1_ref, in_sem.at[chunks + 1]))
    loads.append(pltpu.make_async_copy(w2_hbm, w2_ref, in_sem.at[chunks + 2]))
    for load in loads:
        load.start()

    for c in range(chunks):
        loads[c].wait()

        @pl.loop(0, block_count, unroll=4)
        def _(b):
            block = feats[c][:, lanes(b)]
            locals_[c][b] = block
            tables[c][b] = block

        if c == 0:
            pl.semaphore_wait(barrier, parts + groups - 2)

        @pl.loop(1, parts)
        def _(k):
            peer = lax.rem(me + k, parts)
            for s in range(slots):
                used = (s < cnt_ref[0, peer]).astype(jnp.float32)
                block = locals_[c][sb_ref[0, peer, s]]
                stages[c][peer, s] = (block.astype(jnp.float32) * used).astype(jnp.bfloat16)
            halo_copy(c, peer, me).start()

    for c in range(chunks):
        tables[c][pl.ds(block_count + me * slots, slots)] = jnp.zeros(
            (slots, widths[c], BLOCK), jnp.bfloat16
        )

    gain = 1.0 + eps_ref[0]
    loads[chunks].wait()

    def mixed_block(c, b):
        shape = (widths[c], BLOCK)
        total = gain * feats[c][:, lanes(b)].astype(jnp.float32)
        near = jnp.zeros(shape, jnp.float32)
        degree = jnp.broadcast_to(deg_ref[pl.ds(b, 1), :], shape)
        for j in range(list_width):
            tile = tables[c][tile_ref[j, b]].astype(jnp.float32)
            index = jnp.broadcast_to(nbr_ref[pl.ds(j, 1), lanes(b)], shape)
            taken = jnp.take_along_axis(tile, index, axis=1, mode="promise_in_bounds")
            near = near + jnp.where(degree > j, taken, 0.0)
        return (total + near).astype(jnp.bfloat16)

    for c in range(chunks):
        @pl.loop(1, parts)
        def _(k):
            source = lax.rem(me + k, parts)
            halo_copy(c, source, source).wait_recv()

        span = pl.ds(starts[c], widths[c])
        unroll = per_piece if widths[c] <= 2 * SUBLANES else max(per_piece // 2, 1)

        @pl.loop(0, pieces)
        def _(p):
            for k in range(groups):
                dest = dest_of(k) if k < groups - 1 else z
                first = (dest * pieces + p) * per_piece

                @pl.loop(0, per_piece, unroll=unroll)
                def _(i):
                    block = mixed_block(c, first + i)
                    if k < groups - 1:
                        zstage[p, dest, span, lanes(i)] = block
                    else:
                        parcel[p, z, span, lanes(i)] = block

                if k < groups - 1:
                    row_copy(c, p, dest, z).start()

    loads[chunks + 1].wait()
    loads[chunks + 2].wait()
    depth = w1_ref.shape[0]

    @pl.loop(0, pieces)
    def _(p):
        for c in range(chunks):
            @pl.loop(1, groups)
            def _(k):
                source = lax.rem(z + k, groups)
                row_copy(c, p, source, source).wait_recv()

        columns = parcel[p].reshape(depth, piece_nodes)
        hidden = lax.dot_general(
            columns, w1_ref[...], (((0,), (0,)), ((), ())), preferred_element_type=jnp.float32
        ) + b1_ref[...]
        hidden = jnp.maximum(hidden, 0.0).astype(jnp.bfloat16)
        rows = pl.ds(pl.multiple_of(p * piece_nodes, piece_nodes), piece_nodes)
        out_ref[rows, :] = (
            jnp.dot(hidden, w2_ref[...], preferred_element_type=jnp.float32) + b2_ref[...]
        ).astype(jnp.bfloat16)

    for c in range(chunks):
        @pl.loop(1, parts)
        def _(k):
            halo_copy(c, lax.rem(me + k, parts), me).wait_send()

        @pl.loop(0, pieces)
        def _(p):
            @pl.loop(1, groups)
            def _(k):
                row_copy(c, p, lax.rem(z + k, groups), z).wait_send()


def per_device(
    features, send_blocks, counts, tile_blocks, neighbours, degree, epsilon,
    w_first, b_first, w_second, b_second,
):
    parts = lax.axis_size("dom")
    groups = lax.axis_size("feat")
    cols, rows = features.shape
    slots = send_blocks.shape[2]
    widths = chunk_widths(cols)
    chunks = len(widths)
    block_count = rows // BLOCK
    owned = rows // groups
    pieces = min(PIECES, owned // BLOCK)
    hidden_cols, out_cols = w_second.shape
    depth = w_first.shape[0]
    vmem = pl.BlockSpec(memory_space=pltpu.VMEM)
    smem = pl.BlockSpec(memory_space=pltpu.SMEM)
    anywhere = pl.BlockSpec(memory_space=pl.ANY)
    bf16 = jnp.bfloat16
    return pl.pallas_call(
        functools.partial(kernel, parts, groups, pieces, widths),
        out_shape=pltpu.VMEM((owned, out_cols), bf16),
        in_specs=[smem] * 4 + [vmem] * 3 + [anywhere] * 4,
        out_specs=vmem,
        scratch_shapes=[
            pltpu.VMEM((block_count + parts * slots, w, BLOCK), bf16) for w in widths
        ] + [
            pltpu.VMEM((block_count, w, BLOCK), bf16) for w in widths
        ] + [
            pltpu.VMEM((parts, slots, w, BLOCK), bf16) for w in widths
        ] + [
            pltpu.VMEM((w, rows), bf16) for w in widths
        ] + [
            pltpu.VMEM(neighbours.shape, jnp.int32),
            pltpu.VMEM((depth, hidden_cols), bf16),
            pltpu.VMEM((hidden_cols, out_cols), bf16),
            pltpu.VMEM((pieces, groups, cols, owned // pieces), bf16),
            pltpu.VMEM((pieces, groups, cols, owned // pieces), bf16),
            pltpu.SemaphoreType.DMA((chunks, parts)),
            pltpu.SemaphoreType.DMA((chunks, parts)),
            pltpu.SemaphoreType.DMA((chunks, pieces, groups)),
            pltpu.SemaphoreType.DMA((chunks, pieces, groups)),
            pltpu.SemaphoreType.DMA((chunks + 3,)),
        ],
        compiler_params=pltpu.CompilerParams(
            collective_id=0, has_side_effects=True, vmem_limit_bytes=56 * 1024 * 1024
        ),
    )(
        send_blocks, counts, tile_blocks, epsilon,
        degree.reshape(block_count, BLOCK), b_first.reshape(1, -1), b_second.reshape(1, -1),
        features, neighbours, w_first, w_second,
    )


def solution(mesh):
    return jax.shard_map(
        per_device,
        mesh=mesh,
        in_specs=(
            P("feat", "dom"),
            P("dom", None, None),
            P("dom", None),
            P(None, "dom"),
            P(None, "dom"),
            P("dom"),
            P(), P(), P(), P(), P(),
        ),
        out_specs=P(("dom", "feat"), None),
        check_vma=False,
    )
```

profile of v0, /device:TPU:0, one launch (start us, length us, event | category | flops | bytes accessed | tf_op | source)
XLA Modules:
  0.0 63.5 jit_solution(15372686443954258179)
XLA Ops:
  0.7 61.5 %shard_map.109 = bf16[2048,512]{1,0:T(8,128)(2,1)S(1)} custom-call(s32[1,8,8]{2,1,0:T(8,128)} %sb_ref.1, s32[1,8]{1,0:T(1,128)} %cnt_ref.1, s32[24,64]{1,0:T(8,128)} %tile_ref.1, f32[1]{0:T(128)S(6)} %copy.14.eps_ref, s32[64,128]{1,0:T(8,128)} %bitcast.3, f32[1,512]{1,0:T(1,128)} %bitcast.4, f32[1,512]{1,0:T(1,128)} %bitcast.5, bf16[128,8192]{1,0:T(8,128)(2,1)} %feat_hbm.1, ...), custom_call_target="tpu_custom_call" | custom-call | tf_op jit(solution)/shard_map/pallas_call | solution.py:219
  62.2 1.3 %copy.13 = bf16[2048,512]{1,0:T(8,128)(2,1)} copy(bf16[2048,512]{1,0:T(8,128)(2,1)S(1)} %shard_map.109) | data formatting | bytes 4194304
where the time goes:
time: 63.7 us; the launch traced here: 63.5 us
  Pallas kernels  61.5 us (97%)
  local copies, waits for them, and re-layouts  1.32 us (2%)
  between operations  0.66 us (1%)
    pallas_call x1, Pallas kernels, per_device(): pl.pallas_call(functools.partial(kernel, parts, groups, pieces, widths),...  61.5 us
    unnamed x1, local copies, waits for them, and re-layouts  1.32 us

commit v1 on v0

--- a/solution.py
+++ b/solution.py
@@ -21,7 +21,7 @@
 
 def kernel(
     parts, groups, pieces, widths,
-    sb_ref, cnt_ref, tile_ref, eps_ref, deg_ref, b1_ref, b2_ref,
+    sb_hbm, cnt_hbm, tile_hbm, eps_ref, deg_hbm, b1_hbm, b2_hbm,
     feat_hbm, nbr_hbm, w1_hbm, w2_hbm,
     out_ref,
     *scratch,
@@ -29,7 +29,8 @@
     chunks = len(widths)
     starts = [sum(widths[:c]) for c in range(chunks)]
     tables, locals_, stages, feats = (scratch[i * chunks:(i + 1) * chunks] for i in range(4))
-    (nbr_ref, w1_ref, w2_ref, zstage, parcel,
+    (sb_ref, cnt_ref, tile_ref, deg_ref, b1_ref, b2_ref,
+     nbr_ref, w1_ref, w2_ref, zstage, parcel,
      hsend, hrecv, zsend, zrecv, in_sem) = scratch[4 * chunks:]
     me = lax.axis_index("dom")
     z = lax.axis_index("feat")
@@ -46,8 +47,8 @@
         return pltpu.make_async_remote_copy(
             src_ref=stages[c].at[peer],
             dst_ref=tables[c].at[pl.ds(block_count + source * slots, slots)],
-            send_sem=hsend.at[c, peer],
-            recv_sem=hrecv.at[c, source],
+            send_sem=hsend.at[0],
+            recv_sem=hrecv.at[c],
             device_id={"dom": peer},
             device_id_type=pl.DeviceIdType.MESH,
         )
@@ -57,11 +58,19 @@
         return pltpu.make_async_remote_copy(
             src_ref=zstage.at[p, dest, span],
             dst_ref=parcel.at[p, source, span],
-            send_sem=zsend.at[c, p, dest],
-            recv_sem=zrecv.at[c, p, source],
+            send_sem=zsend.at[0],
+            recv_sem=zrecv.at[p],
             device_id={"feat": dest},
             device_id_type=pl.DeviceIdType.MESH,
         )
+
+    def halo_all(c, sem):
+        blocks = tables[c].at[pl.ds(0, (parts - 1) * slots)]
+        return pltpu.make_async_copy(blocks, blocks, sem)
+
+    def row_all(p, sem):
+        rows = parcel.at[p, pl.ds(0, groups - 1)]
+        return pltpu.make_async_copy(rows, rows, sem)
 
     def dest_of(k):
         if k < half:
@@ -90,11 +99,26 @@
         )
         for c in range(chunks)
     ]
-    loads.append(pltpu.make_async_copy(nbr_hbm, nbr_ref, in_sem.at[chunks]))
-    loads.append(pltpu.make_async_copy(w1_hbm, w1_ref, in_sem.at[chunks + 1]))
-    loads.append(pltpu.make_async_copy(w2_hbm, w2_ref, in_sem.at[chunks + 2]))
-    for load in loads:
+    small = [
+        pltpu.make_async_copy(source, target, in_sem.at[chunks])
+        for source, target in ((sb_hbm, sb_ref), (cnt_hbm, cnt_ref))
+    ]
+    lists = [
+        pltpu.make_async_copy(source, target, in_sem.at[chunks + 1])
+        for source, target in (
+            (tile_hbm, tile_ref), (deg_hbm, deg_ref), (nbr_hbm, nbr_ref),
+        )
+    ]
+    weights = [
+        pltpu.make_async_copy(source, target, in_sem.at[chunks + 2])
+        for source, target in (
+            (w1_hbm, w1_ref), (w2_hbm, w2_ref), (b1_hbm, b1_ref), (b2_hbm, b2_ref),
+        )
+    ]
+    for load in loads[:1] + small + loads[1:] + lists + weights:
         load.start()
+    for load in small:
+        load.wait()
 
     for c in range(chunks):
         loads[c].wait()
@@ -122,8 +146,9 @@
             (slots, widths[c], BLOCK), jnp.bfloat16
         )
 
+    for load in lists:
+        load.wait()
     gain = 1.0 + eps_ref[0]
-    loads[chunks].wait()
 
     def mixed_block(c, b):
         shape = (widths[c], BLOCK)
@@ -138,10 +163,7 @@
         return (total + near).astype(jnp.bfloat16)
 
     for c in range(chunks):
-        @pl.loop(1, parts)
-        def _(k):
-            source = lax.rem(me + k, parts)
-            halo_copy(c, source, source).wait_recv()
+        halo_all(c, hrecv.at[c]).wait()
 
         span = pl.ds(starts[c], widths[c])
         unroll = per_piece if widths[c] <= 2 * SUBLANES else max(per_piece // 2, 1)
@@ -163,18 +185,15 @@
                 if k < groups - 1:
                     row_copy(c, p, dest, z).start()
 
-    loads[chunks + 1].wait()
-    loads[chunks + 2].wait()
+    for load in weights:
+        load.wait()
+    for c in range(chunks):
+        halo_all(c, hsend.at[0]).wait()
     depth = w1_ref.shape[0]
 
     @pl.loop(0, pieces)
     def _(p):
-        for c in range(chunks):
-            @pl.loop(1, groups)
-            def _(k):
-                source = lax.rem(z + k, groups)
-                row_copy(c, p, source, source).wait_recv()
-
+        row_all(p, zrecv.at[p]).wait()
         columns = parcel[p].reshape(depth, piece_nodes)
         hidden = lax.dot_general(
             columns, w1_ref[...], (((0,), (0,)), ((), ())), preferred_element_type=jnp.float32
@@ -185,16 +204,8 @@
             jnp.dot(hidden, w2_ref[...], preferred_element_type=jnp.float32) + b2_ref[...]
         ).astype(jnp.bfloat16)
 
-    for c in range(chunks):
-        @pl.loop(1, parts)
-        def _(k):
-            halo_copy(c, lax.rem(me + k, parts), me).wait_send()
-
-        @pl.loop(0, pieces)
-        def _(p):
-            @pl.loop(1, groups)
-            def _(k):
-                row_copy(c, p, lax.rem(z + k, groups), z).wait_send()
+    for p in range(pieces):
+        row_all(p, zsend.at[0]).wait()
 
 
 def per_device(
@@ -213,13 +224,13 @@
     hidden_cols, out_cols = w_second.shape
     depth = w_first.shape[0]
     vmem = pl.BlockSpec(memory_space=pltpu.VMEM)
+    hbm = pl.BlockSpec(memory_space=pltpu.HBM)
     smem = pl.BlockSpec(memory_space=pltpu.SMEM)
-    anywhere = pl.BlockSpec(memory_space=pl.ANY)
     bf16 = jnp.bfloat16
     return pl.pallas_call(
         functools.partial(kernel, parts, groups, pieces, widths),
         out_shape=pltpu.VMEM((owned, out_cols), bf16),
-        in_specs=[smem] * 4 + [vmem] * 3 + [anywhere] * 4,
+        in_specs=[hbm] * 3 + [smem] + [hbm] * 7,
         out_specs=vmem,
         scratch_shapes=[
             pltpu.VMEM((block_count + parts * slots, w, BLOCK), bf16) for w in widths
@@ -230,15 +241,21 @@
         ] + [
             pltpu.VMEM((w, rows), bf16) for w in widths
         ] + [
+            pltpu.SMEM(send_blocks.shape, jnp.int32),
+            pltpu.SMEM(counts.shape, jnp.int32),
+            pltpu.SMEM(tile_blocks.shape, jnp.int32),
+            pltpu.VMEM((block_count, BLOCK), jnp.int32),
+            pltpu.VMEM((1, hidden_cols), jnp.float32),
+            pltpu.VMEM((1, out_cols), jnp.float32),
             pltpu.VMEM(neighbours.shape, jnp.int32),
             pltpu.VMEM((depth, hidden_cols), bf16),
             pltpu.VMEM((hidden_cols, out_cols), bf16),
             pltpu.VMEM((pieces, groups, cols, owned // pieces), bf16),
             pltpu.VMEM((pieces, groups, cols, owned // pieces), bf16),
-            pltpu.SemaphoreType.DMA((chunks, parts)),
-            pltpu.SemaphoreType.DMA((chunks, parts)),
-            pltpu.SemaphoreType.DMA((chunks, pieces, groups)),
-            pltpu.SemaphoreType.DMA((chunks, pieces, groups)),
+            pltpu.SemaphoreType.DMA((1,)),
+            pltpu.SemaphoreType.DMA((chunks,)),
+            pltpu.SemaphoreType.DMA((1,)),
+            pltpu.SemaphoreType.DMA((pieces,)),
             pltpu.SemaphoreType.DMA((chunks + 3,)),
         ],
         compiler_params=pltpu.CompilerParams(

time: 63.7 us -> 59.9 us (0.940)
  Pallas kernels: 61.5 us -> 57.8 us
    pallas_call x1, Pallas kernels: 61.5 us -> 57.8 us  [per_device(): pl.pallas_call(functools.partial(kernel, parts, groups, pieces, widths),...]
where the time goes in v1:
time: 59.9 us; the launch traced here: 59.7 us
  Pallas kernels  57.8 us (96%)
  local copies, waits for them, and re-layouts  1.32 us (2%)
  between operations  0.66 us (1%)
    pallas_call x1, Pallas kernels, per_device(): pl.pallas_call(functools.partial(kernel, parts, groups, pieces, widths),...  57.8 us
    unnamed x1, local copies, waits for them, and re-layouts  1.32 us

profile of v1, /device:TPU:0, one launch (start us, length us, event | category | flops | bytes accessed | tf_op | source)
XLA Modules:
  0.0 59.7 jit_solution(14933019649307995512)
XLA Ops:
  0.7 57.8 %shard_map.109 = bf16[2048,512]{1,0:T(8,128)(2,1)S(1)} custom-call(s32[1,8,8]{2,1,0:T(8,128)} %sb_hbm.1, s32[1,8]{1,0:T(1,128)} %cnt_hbm.1, s32[24,64]{1,0:T(8,128)} %tile_hbm.1, f32[1]{0:T(128)S(6)} %copy.14.eps_ref, s32[64,128]{1,0:T(8,128)} %bitcast.3, f32[1,512]{1,0:T(1,128)} %bitcast.4, f32[1,512]{1,0:T(1,128)} %bitcast.5, bf16[128,8192]{1,0:T(8,128)(2,1)} %feat_hbm.1, ...), custom_call_target="tpu_custom_call" | custom-call | tf_op jit(solution)/shard_map/pallas_call | solution.py:230
  58.4 1.3 %copy.13 = bf16[2048,512]{1,0:T(8,128)(2,1)} copy(bf16[2048,512]{1,0:T(8,128)(2,1)S(1)} %shard_map.109) | data formatting | bytes 4194304
